TPU v7x, 32 devices: a whole 2x2x4 slice. The times are simulated.
32 devices in a mesh: dp: 8 (over z, x), expert: 4 (over y, core).
Axes of the slice: x: 2, y: 2, z: 4, core: 2. Of those that a mesh axis runs over, the one named last changes fastest.
Arguments:
- queries: bfloat16 [256, 2048], P(('dp', 'expert')), may hold values from -8 to 8
- fresh_key: bfloat16 [256, 256], P(('dp', 'expert')), may hold values from -4 to 4
- fresh_value: bfloat16 [256, 256], P(('dp', 'expert')), may hold values from -4 to 4
- cached_keys: bfloat16 [256, 128, 256], P(('dp', 'expert')), may hold values from -8 to 8
- cached_values: bfloat16 [256, 128, 256], P(('dp', 'expert')), may hold values from -4 to 4
- lengths: int32 [256], P(('dp', 'expert')), may hold values from 2 to 128
- sink_logit_rows: float32 [32], replicated, may hold values from 1 to 5
- residual: bfloat16 [256, 2880], P('dp', 'expert'), may hold values from -6 to 6
- o_weight: bfloat16 [2880, 2048], P('expert'), may hold values from -0.125 to 0.125
- norm_gain: float32 [2880], replicated, may hold values from 0.5 to 1.5
- expert_ids: int32 [256, 4], replicated, may hold values from 0 to 7, all different within a row; in each aligned block of 32 rows (0 to 31, 32 to 63, ...) at most 32 rows name the same one
- route_weights: float32 [256, 4], replicated, may hold values from 0.1 to 0.6
- w_gate_up: bfloat16 [8, 2, 2880, 2880], P('dp', None, 'expert'), may hold values from -0.109375 to 0.109375
- w_down: bfloat16 [8, 2880, 2880], P('dp', 'expert'), may hold values from -0.15625 to 0.15625
Outputs:
- layer_out: bfloat16 [256, 2880], P('dp', 'expert')
Inputs may be any that keep to these rules, and one draw needn't show every extreme that they name: `expert_ids`: each row names 4 different experts; among any aligned block of 32 rows no expert is named by more than 32 rows.
All inputs are finite; a program needn't handle non-finite values.
Results may differ from a plain program's by a relative error of at most 0.018.
Values may be sent and summed in bfloat16 or wider, within the bound.
No kernel may reach another device: no remote copies, remote signals or barrier semaphores. Data moves between devices by JAX's collectives and lax.ppermute only.
A program may use at most 64 MiB of HBM per device.

v0:
```python
import math
import jax
import jax.numpy as jnp
from jax import lax
from jax.sharding import PartitionSpec as P

D = 2880
QUERY_HEADS = 32
KEY_VALUE_HEADS = 4
HEAD_SIZE = 64
WINDOW_LENGTH = 128
TOP = 4
norm_eps = 1e-05
swish_alpha = 1.702


def attend(queries, fresh_key, fresh_value, cached_keys, cached_values, lengths, sink_logit_rows):
    batch_count = queries.shape[0]
    head_groups = QUERY_HEADS // KEY_VALUE_HEADS
    query_head_rows = queries.reshape(batch_count, KEY_VALUE_HEADS, head_groups, HEAD_SIZE)
    key_rows = cached_keys.reshape(batch_count, WINDOW_LENGTH, KEY_VALUE_HEADS, HEAD_SIZE)
    value_rows = cached_values.reshape(batch_count, WINDOW_LENGTH, KEY_VALUE_HEADS, HEAD_SIZE)
    score_scale = 1.0 / math.sqrt(HEAD_SIZE)
    cache_scores = (
        jnp.einsum("bkgd,bwkd->bkgw", query_head_rows, key_rows, preferred_element_type=jnp.float32)
        * score_scale
    )
    own_scores = (
        jnp.einsum(
            "npwm,npm->npw",
            query_head_rows,
            fresh_key.reshape(batch_count, KEY_VALUE_HEADS, HEAD_SIZE),
            preferred_element_type=jnp.float32,
        )
        * score_scale
    )
    slots = jnp.arange(WINDOW_LENGTH, dtype=jnp.int32)
    valid = (slots[None, :] >= (WINDOW_LENGTH - lengths)[:, None])[:, None, None, :]
    sink_terms = sink_logit_rows.reshape(KEY_VALUE_HEADS, head_groups)[None]
    masked = jnp.where(valid, cache_scores, -jnp.inf)
    top = jnp.maximum(jnp.maximum(jnp.max(masked, axis=-1), own_scores), sink_terms)
    cache_exp = jnp.where(valid, jnp.exp(masked - top[..., None]), 0.0)
    self_exp = jnp.exp(own_scores - top)
    total = jnp.sum(cache_exp, axis=-1) + self_exp + jnp.exp(sink_terms - top)
    cache_prob = (cache_exp / total[..., None]).astype(jnp.bfloat16)
    own_probability = (self_exp / total).astype(jnp.bfloat16)
    blended = jnp.einsum(
        "bkgw,bwkd->bkgd", cache_prob, value_rows, preferred_element_type=jnp.float32
    )
    blended = blended + own_probability.astype(jnp.float32)[..., None] * fresh_value.reshape(
        batch_count, KEY_VALUE_HEADS, 1, HEAD_SIZE
    ).astype(jnp.float32)
    return blended.reshape(batch_count, QUERY_HEADS * HEAD_SIZE).astype(jnp.bfloat16)


def slot_onehot(named, capacity):
    counts = jnp.cumsum(named.astype(jnp.int32), axis=1) - 1
    places = jnp.arange(capacity, dtype=jnp.int32)
    return named[:, None, :] & (counts[:, None, :] == places[None, :, None])


def receiver_slots(expert_ids, route_weights, expert, blocks, capacity):
    picked = expert_ids == expert
    named = jnp.any(picked, axis=1).reshape(blocks, -1)
    weight_at = jnp.sum(jnp.where(picked, route_weights, 0.0), axis=1).reshape(blocks, -1)
    onehot = slot_onehot(named, capacity)
    slot_weight = jnp.sum(jnp.where(onehot, weight_at[:, None, :], 0.0), axis=2)
    return (onehot, slot_weight)


def sender_slots(my_ids, experts, capacity):
    labels = jnp.arange(experts, dtype=jnp.int32)
    named = jnp.any(my_ids[None, :, :] == labels[:, None, None], axis=2)
    return slot_onehot(named, capacity)


def body(
    queries,
    fresh_key,
    fresh_value,
    cached_keys,
    cached_values,
    lengths,
    sink_logit_rows,
    residual,
    o_weight,
    norm_gain,
    expert_ids,
    route_weights,
    w_gate_up,
    w_down,
):
    attended = attend(
        queries, fresh_key, fresh_value, cached_keys, cached_values, lengths, sink_logit_rows
    )
    projected = lax.dot_general(
        lax.all_gather(attended, "expert", axis=0, tiled=True),
        o_weight,
        (((1,), (1,)), ((), ())),
        preferred_element_type=jnp.float32,
    )
    stream = (residual.astype(jnp.float32) + projected).astype(jnp.bfloat16)
    wide = stream.astype(jnp.float32)
    group_rows = stream.shape[0]
    columns = stream.shape[1]
    experts = lax.axis_size("dp")
    capacity = 2 * group_rows * TOP // experts
    gain_cols = lax.dynamic_slice_in_dim(norm_gain, lax.axis_index("expert") * columns, columns)
    squares = lax.psum(jnp.sum(wide * wide, axis=1), "expert")
    score_scale = lax.rsqrt(squares / D + norm_eps)
    outgoing = (wide * score_scale[:, None] * gain_cols[None, :]).astype(jnp.bfloat16)
    onehot_in, slot_weight = receiver_slots(
        expert_ids, route_weights, lax.axis_index("dp"), experts, capacity
    )
    my_ids = lax.dynamic_slice_in_dim(expert_ids, lax.axis_index("dp") * group_rows, group_rows, 0)
    onehot_out = sender_slots(my_ids, experts, capacity)
    outbound = jnp.einsum(
        "ect,td->ecd", onehot_out.astype(jnp.bfloat16), outgoing, preferred_element_type=jnp.float32
    ).astype(jnp.bfloat16)
    received = lax.all_to_all(outbound, "dp", split_axis=0, concat_axis=0, tiled=True)
    rows = received.reshape(experts * capacity, columns)
    gate_up = w_gate_up[0]
    down = w_down[0]
    both = jnp.einsum(
        "rc,hfc->rhf",
        lax.all_gather(rows, "expert", axis=1, tiled=True),
        gate_up,
        preferred_element_type=jnp.float32,
    )
    gate = both[:, 0]
    up = both[:, 1]
    hidden = ((up + 1.0) * gate * jax.nn.sigmoid(swish_alpha * gate)).astype(jnp.bfloat16)
    summed = lax.psum_scatter(
        lax.dot_general(
            down, hidden, (((0,), (1,)), ((), ())), preferred_element_type=jnp.float32
        ).astype(jnp.bfloat16),
        "expert",
        scatter_dimension=0,
        tiled=True,
    ).astype(jnp.float32)
    contribution = (summed * slot_weight.reshape(1, -1)).astype(jnp.bfloat16)
    contribution = contribution.T.reshape(experts, capacity, columns)
    returned = lax.all_to_all(contribution, "dp", split_axis=0, concat_axis=0, tiled=True)
    returned_sum = jnp.einsum(
        "ect,ecd->td",
        onehot_out.astype(jnp.float32),
        returned.astype(jnp.float32),
        precision=lax.Precision.HIGHEST,
    )
    return (wide + returned_sum).astype(jnp.bfloat16)


def solution(mesh):
    placed = (
        P(("dp", "expert"), None),
        P(("dp", "expert"), None),
        P(("dp", "expert"), None),
        P(("dp", "expert"), None, None),
        P(("dp", "expert"), None, None),
        P(("dp", "expert")),
        P(),
        P("dp", "expert"),
        P("expert", None),
        P(),
        P(),
        P(),
        P("dp", None, "expert", None),
        P("dp", "expert", None),
    )
    return jax.shard_map(
        body, mesh=mesh, in_specs=placed, out_specs=P("dp", "expert"), check_vma=False
    )
```

profile of v0, /device:TPU:0, one launch (start us, length us, event | category | flops | bytes accessed | tf_op | source)
XLA Modules:
  0.0 138.2 jit_solution(12964307490870638373)
XLA Ops:
  6.5 0.0 copy-start
  6.5 0.0 all-gather.2.cloned.1.call-start
  6.5 0.8 broadcast_subtract_fusion
  7.4 0.1 iota_compare_fusion.3
  7.4 0.9 reshape.81
  8.4 1.3 copy.27
  9.7 1.4 reshape.94
  11.1 0.7 max.14
  11.8 0.9 fusion.48
  12.7 0.3 fusion.47
  13.0 0.2 fusion.28
  13.2 0.4 copy-done.1
  13.6 0.6 fusion.42
  14.3 1.3 copy.28
  15.6 0.0 copy-done.4
  15.6 0.7 reshape.87
  16.3 0.0 copy-done.3
  16.3 1.4 %fusion.12 = bf16[8,4,8,64]{3,2,1,0:T(8,128)(2,1)S(1)} fusion(bf16[8,128,4,64]{1,3,2,0:T(8,128)(2,1)S(1)} %bitcast.48, f32[8,4,8,128]{3,2,1,0:T(8,128)} %copy-done.1, f32[8,4,64]{2,1,0:T(4,128)} %reshape.87, f32[8,4,8]{2,1,0:T(4,128)} %get-tuple-element.7, f32[8,4,8]{2,1,0:T(4,128)} %get-tuple-element.8, f32[8,4,8]{2,1,0:T(4,128)S(1)} %maximum_maximum_fusion, ...), kind=kOutput, calls=%fused_computation.11 | convolution fusion | flops 4374528 | bytes 700416 | tf_op jit(solution)/shard_map/bkgw,bwkd->bkgd/dot_general | solution.py:47
  17.7 0.1 convert_element_type.86
  17.8 6.5 %all_gather.6 = bf16[32,2048]{1,0:T(8,128)(2,1)S(1)} all-gather(bf16[8,2048]{1,0:T(8,128)(2,1)S(1)} %convert_element_type.86), channel_id=1, replica_groups=mesh['dp'=8,'expert'=4] {'expert'}, dimensions={0}, use_global_device_ids=true | all-gather | bytes 163840 | tf_op jit(solution)/shard_map/all_gather | solution.py:97
  24.4 0.0 copy-done
  24.4 1.9 %multiply_reduce_fusion = (f32[32]{0:T(128)S(1)}, f32[32,720]{1,0:T(8,128)S(1)}) fusion(bf16[32,2048]{1,0:T(8,128)(2,1)S(1)} %all_gather.6, bf16[720,2048]{1,0:T(8,128)(2,1)S(1)} %copy-done, bf16[32,720]{1,0:T(8,128)(2,1)} %param.21), kind=kOutput, calls=%fused_computation.35 | convolution fusion | flops 94510048 | bytes 3218560 | tf_op jit(solution)/shard_map/dot_general | solution.py:96
  26.2 7.5 %psum.7 = f32[32]{0:T(128)S(1)} all-reduce(f32[32]{0:T(128)S(1)} %get-tuple-element.11), channel_id=1, replica_groups=mesh['dp'=8,'expert'=4] {'expert'}, use_global_device_ids=true, to_apply=%region_5.6 | all-reduce | flops 32 | bytes 256 | tf_op jit(solution)/shard_map/psum | solution.py:109
  33.7 0.8 constant_dynamic-slice_fusion
  34.5 0.2 reduce_window_sum.17
  34.7 0.8 dynamic_slice.7
  35.4 0.4 convolution_convert_fusion
  35.8 16.2 %all_to_all.10 = bf16[8,32,720]{2,1,0:T(8,128)(2,1)S(1)} all-to-all(bf16[8,32,720]{2,1,0:T(8,128)(2,1)S(1)} %convolution_convert_fusion), channel_id=1, replica_groups=mesh['dp'=8,'expert'=4] {'dp'}, dimensions={0} | all-to-all | bytes 737280 | tf_op jit(solution)/shard_map/all_to_all | solution.py:120
  52.1 0.9 copy.30
  53.0 0.0 all-gather.2.cloned.1.call-update
  53.0 0.0 reduce-scatter.2.cloned.1.call-start
  53.1 17.9 %all-gather.2.cloned.1.call-done = bf16[256,2880]{0,1:T(8,128)(2,1)} async-done(((bf16[256,720]{0,1:T(8,128)(2,1)}), bf16[256,2880]{0,1:T(8,128)(2,1)}) %all-gather.2.cloned.1.call-update) | async-done | bytes 1474576 | tf_op jit(solution)/shard_map/all_gather | solution.py:126
  71.0 6.3 %fusion = f32[256,2,720]{0,2,1:T(8,128)S(1)} fusion(bf16[1,2,720,2880]{3,2,1,0:T(8,128)(2,1)} %param.26, bf16[256,2880]{0,1:T(8,128)(2,1)} %all-gather.2.cloned.1.call-done), kind=kOutput, calls=%fused_computation | convolution fusion | flops 2123366400 | bytes 11243520 | tf_op jit(solution)/shard_map/rc,hfc->rhf/dot_general | solution.py:124
  77.3 0.0 copy-start.2
  77.3 0.0 copy-start.5
  77.3 5.3 %fusion.7 = bf16[2880,256]{1,0:T(8,128)(2,1)} fusion(bf16[1,720,2880]{2,1,0:T(8,128)(2,1)} %param.27, f32[256,2,720]{0,2,1:T(8,128)S(1)} %fusion), kind=kOutput, calls=%fused_computation.5 | convolution fusion | flops 1063895040 | bytes 7096320 | tf_op jit(solution)/shard_map/dot_general | solution.py:134
  82.6 0.0 reduce-scatter.2.cloned.1.call-update
  82.6 0.0 copy-done.2
  82.6 0.1 and.22
  82.7 0.2 reduce_window_sum.18
  83.0 0.1 broadcast_in_dim.55
  83.0 0.1 select_reduce_fusion
  83.2 0.1 mul.93
  83.2 27.0 %reduce-scatter.2.cloned.1.call-done = bf16[720,256]{1,0:T(8,128)(2,1)} async-done(((bf16[2880,256]{1,0:T(8,128)(2,1)}), bf16[720,256]{1,0:T(8,128)(2,1)}) %reduce-scatter.2.cloned.1.call-update) | async-done | bytes 368656 | tf_op jit(solution)/shard_map/reduce_scatter | solution.py:133
  110.2 1.8 %fusion.20 = bf16[256,720]{0,1:T(8,128)(2,1)} fusion(bf16[720,256]{1,0:T(8,128)(2,1)} %reduce-scatter.2.cloned.1.call-done, f32[256]{0:T(256)S(1)} %mul.93), kind=kLoop, calls=%fused_computation.23 | loop fusion | flops 552960 | bytes 738304 | tf_op jit(solution)/shard_map/transpose | solution.py:142
  112.0 1.2 copy.31
  113.2 17.2 %all_to_all.11 = bf16[8,32,720]{2,1,0:T(8,128)(2,1)S(1)} all-to-all(bf16[8,32,720]{2,1,0:T(8,128)(2,1)S(1)} %bitcast.47), channel_id=1, replica_groups=mesh['dp'=8,'expert'=4] {'dp'}, dimensions={0} | all-to-all | bytes 737280 | tf_op jit(solution)/shard_map/all_to_all | solution.py:143
  130.4 1.0 fusion.16
  (13 shorter events, 0.1 us)
Async XLA Ops:
  6.5 17.8 %copy-start = (bf16[720,2048]{1,0:T(8,128)(2,1)S(1)}, bf16[720,2048]{1,0:T(8,128)(2,1)}, u32[]{:S(2)}) copy-start(bf16[720,2048]{1,0:T(8,128)(2,1)} %param.22) | copy-start | bytes 8847364
  6.5 9.1 %copy-start.4 = (bf16[8,256]{1,0:T(8,128)(2,1)S(1)}, bf16[8,256]{1,0:T(8,128)(2,1)}, u32[]{:S(2)}) copy-start(bf16[8,256]{1,0:T(8,128)(2,1)} %param.16) | copy-start | bytes 12292
  6.5 64.4 %all-gather.2.cloned.1.call-start = ((), (), s32[]{:S(2)}) async-start(), calls=%async_computation.3 | async-start | bytes 1843200 | tf_op jit(solution)/shard_map/all_gather | solution.py:126
  7.4 8.9 %copy-start.3 = (pred[8,128]{1,0:T(8,128)(4,1)}, pred[8,128]{1,0:T(8,128)(4,1)S(1)}, u32[]{:S(2)}) copy-start(pred[8,128]{1,0:T(8,128)(4,1)S(1)} %iota_compare_fusion.3) | copy-start | bytes 3076
  13.0 0.6 copy-start.1
  53.0 57.2 %reduce-scatter.2.cloned.1.call-start = ((), (), s32[]{:S(2)}) async-start(), calls=%async_computation.4 | async-start | bytes 1843200 | tf_op jit(solution)/shard_map/reduce_scatter | solution.py:133
  77.3 5.3 %copy-start.2 = (s32[256,4]{0,1:T(4,128)S(1)}, s32[256,4]{0,1:T(4,128)}, u32[]{:S(2)}) copy-start(s32[256,4]{0,1:T(4,128)} %param.24) | copy-start | bytes 12292
  77.3 5.6 %copy-start.5 = (f32[256,4]{0,1:T(4,128)S(1)}, f32[256,4]{0,1:T(4,128)}, u32[]{:S(2)}) copy-start(f32[256,4]{0,1:T(4,128)} %param.25) | copy-start | bytes 12292
Sparse Core Ops, SparseCore 0:
  53.1 17.7 all-gather.1
  82.7 27.4 reduce-scatter.1
where the time goes:
time: 139 us; the launch traced here: 138 us
  blocking collectives  47.5 us (34%)
  waiting for transfers between devices  44.9 us (32%)
  matrix products  17.4 us (13%)
  between operations  13.5 us (10%)
  local copies, waits for them, and re-layouts  10.8 us (8%)
  other arithmetic  4.1 us (3%)
    reduce_scatter x1, waiting for transfers between devices, body(): lax.psum_scatter(lax.dot_general(down, hidden, (((0,), (1,)), ((), ())),...  27 us
    all_gather x1, waiting for transfers between devices, body(): lax.all_gather(rows, 'expert', axis=1, tiled=True)  17.9 us
    all_to_all x1, blocking collectives, body(): lax.all_to_all(contribution, 'dp', split_axis=0, concat_axis=0, tiled=True)  17.2 us
    all_to_all x1, blocking collectives, body(): lax.all_to_all(outbound, 'dp', split_axis=0, concat_axis=0, tiled=True)  16.2 us
    psum x1, blocking collectives, body(): squares = lax.psum(jnp.sum(wide * wide, axis=1), 'expert')  7.47 us
    all_gather x1, blocking collectives, body(): lax.all_gather(attended, 'expert', axis=0, tiled=True)  6.54 us
    dot_general x1, matrix products, body(): jnp.einsum('rc,hfc->rhf', lax.all_gather(rows, 'expert', axis=1, tiled=Tr...  6.32 us
    dot_general x1, matrix products, body(): lax.dot_general(down, hidden, (((0,), (1,)), ((), ())), preferred_element...  5.28 us
  transfers between devices with their start and end apart: 2, of which 2 were waited for; matrix products, arithmetic and copies ran while one was open for 0% of the time, Pallas kernels for 0%

commit v1 on v0

--- a/solution.py
+++ b/solution.py
@@ -121,11 +121,38 @@
     rows = received.reshape(experts * capacity, columns)
     gate_up = w_gate_up[0]
     down = w_down[0]
-    both = jnp.einsum(
-        "rc,hfc->rhf",
-        lax.all_gather(rows, "expert", axis=1, tiled=True),
-        gate_up,
-        preferred_element_type=jnp.float32,
+
+    def place_pipes_all(message, vals):
+        local_next, right_arr, everything = (
+            lax.axis_size("expert"),
+            lax.axis_index("expert"),
+            message.shape[1],
+        )
+        views = [(num, (num + 1) % local_next) for num in range(local_next)]
+        pages = [(num, (num - 1) % local_next) for num in range(local_next)]
+        mat_out = local_next // 2
+        long_array = w1 = message
+        block_last = vals(message, right_arr * everything)
+        i0 = 1
+        while i0 < mat_out + 1:
+            long_array = lax.ppermute(long_array, "expert", views)
+            if i0 < local_next - mat_out:
+                w1 = lax.ppermute(w1, "expert", pages)
+                reply = vals(w1, (right_arr + i0) % local_next * everything)
+                block_last = block_last + reply
+            block_out = vals(long_array, (right_arr - i0) % local_next * everything)
+            block_last = block_last + block_out
+            i0 = i0 + 1
+        return block_last
+
+    both = place_pipes_all(
+        rows,
+        lambda shard, offset: jnp.einsum(
+            "rc,hfc->rhf",
+            shard,
+            lax.dynamic_slice_in_dim(gate_up, offset, shard.shape[1], axis=2),
+            preferred_element_type=jnp.float32,
+        ),
     )
     gate = both[:, 0]
     up = both[:, 1]

time: 139 us -> 130 us (0.935)
  waiting for transfers between devices: 44.9 us -> 32.6 us
  matrix products: 17.4 us -> 20.4 us
  starting transfers between devices: 0.04 us -> 2.05 us
    all_gather x1 -> x0, waiting for transfers between devices: 17.9 us -> none  [body(): lax.all_gather(rows, 'expert', axis=1, tiled=True)]
    ppermute x0 -> x3, waiting for transfers between devices: none -> 5.87 us  [the longest x2 5.86 us: place_pipes_all(): long_array = lax.ppermute(long_array, 'expert', views)]
    dot_general x1 -> x4, matrix products: 6.32 us -> 11.4 us  [body(): jnp.einsum('rc,hfc->rhf', shard, lax.dynamic_slice_in_dim(gate_up, offset...]
    dot_general x1, matrix products: 5.28 us -> 3.16 us  [body(): lax.dot_general(down, hidden, (((0,), (1,)), ((), ())), preferred_element...]
    ppermute x0 -> x3, starting transfers between devices: none -> 2.05 us  [the longest x1 1.74 us: place_pipes_all(): w1 = lax.ppermute(w1, 'expert', pages)]
    unnamed x14 -> x16, local copies, waits for them, and re-layouts: 3.05 us -> 3.54 us
  transfers between devices with their start and end apart: 2 -> 4, of which waited for: 2 -> 3; matrix products, arithmetic and copies ran while one was open for 0% -> 7% of each run, Pallas kernels for 0% -> 0%
where the time goes in v1:
time: 130 us; the launch traced here: 129 us
  blocking collectives  47.5 us (37%)
  waiting for transfers between devices  32.6 us (25%)
  matrix products  20.4 us (16%)
  between operations  13.6 us (10%)
  local copies, waits for them, and re-layouts  9.86 us (8%)
  other arithmetic  3.35 us (3%)
  starting transfers between devices  2.05 us (2%)
    reduce_scatter x1, waiting for transfers between devices, body(): lax.psum_scatter(lax.dot_general(down, hidden, (((0,), (1,)), ((), ())),...  26.7 us
    all_to_all x1, blocking collectives, body(): lax.all_to_all(contribution, 'dp', split_axis=0, concat_axis=0, tiled=True)  17.3 us
    all_to_all x1, blocking collectives, body(): lax.all_to_all(outbound, 'dp', split_axis=0, concat_axis=0, tiled=True)  16.2 us
    dot_general x4, matrix products, body(): jnp.einsum('rc,hfc->rhf', shard, lax.dynamic_slice_in_dim(gate_up, offset...  11.4 us
    psum x1, blocking collectives, body(): squares = lax.psum(jnp.sum(wide * wide, axis=1), 'expert')  7.48 us
    all_gather x1, blocking collectives, body(): lax.all_gather(attended, 'expert', axis=0, tiled=True)  6.54 us
    ppermute x2, waiting for transfers between devices, place_pipes_all(): long_array = lax.ppermute(long_array, 'expert', views)  5.86 us
    unnamed x16, local copies, waits for them, and re-layouts  3.54 us
  transfers between devices with their start and end apart: 4, of which 3 were waited for; matrix products, arithmetic and copies ran while one was open for 7% of the time, Pallas kernels for 0%

profile of v1, /device:TPU:0, one launch (start us, length us, event | category | flops | bytes accessed | tf_op | source)
XLA Modules:
  0.0 129.3 jit_solution(2684317064069445579)
XLA Ops:
  6.6 2.2 %copy.32 = bf16[8,128,256]{1,2,0:T(8,128)(2,1)} copy(bf16[8,128,256]{2,1,0:T(8,128)(2,1)} %param.18) | data formatting | bytes 1048576 | tf_op args[4]
  8.7 0.9 reshape.85
  9.6 1.3 %copy.31 = bf16[8,128,256]{1,2,0:T(8,128)(2,1)S(1)} copy(bf16[8,128,256]{2,1,0:T(8,128)(2,1)} %param.17) | data formatting | bytes 1048576 | tf_op args[3]
  11.0 0.7 broadcast_subtract_fusion
  11.6 0.1 iota_compare_fusion.3
  11.7 1.4 %reshape.91 = f32[8,4,64]{2,1,0:T(4,128)} reshape(bf16[8,256]{1,0:T(8,128)(2,1)} %param.16) | data formatting | bytes 12288 | tf_op jit(solution)/shard_map/convert_element_type | solution.py:52
  13.1 0.7 reshape.101
  13.8 0.1 max.14
  13.8 0.9 fusion.66
  14.7 0.3 fusion.65
  15.1 0.2 fusion.42
  15.3 1.5 %fusion.23 = bf16[8,4,8,64]{3,2,1,0:T(8,128)(2,1)S(1)} fusion(bf16[8,128,4,64]{1,3,2,0:T(8,128)(2,1)} %bitcast.69, f32[8,4,8,128]{3,2,1,0:T(8,128)S(1)} %get-tuple-element.10, f32[8,4,64]{2,1,0:T(4,128)} %reshape.91, f32[8,4,8]{2,1,0:T(4,128)S(1)} %get-tuple-element.7, f32[8,4,8]{2,1,0:T(4,128)S(1)} %get-tuple-element.8, ...), kind=kOutput, calls=%fused_computation.21 | convolution fusion | flops 4374528 | bytes 700416 | tf_op jit(solution)/shard_map/bkgw,bwkd->bkgd/dot_general | solution.py:47
  16.8 0.1 convert_element_type.86
  17.0 6.5 %all_gather.3 = bf16[32,2048]{1,0:T(8,128)(2,1)S(1)} all-gather(bf16[8,2048]{1,0:T(8,128)(2,1)S(1)} %convert_element_type.86), channel_id=1, replica_groups=mesh['dp'=8,'expert'=4] {'expert'}, dimensions={0}, use_global_device_ids=true | all-gather | bytes 163840 | tf_op jit(solution)/shard_map/all_gather | solution.py:97
  23.5 0.0 copy-done.1
  23.5 0.1 constant_dynamic-slice_fusion
  23.6 0.2 reduce_window_sum.17
  23.8 1.9 %multiply_reduce_fusion = (f32[32]{0:T(128)S(1)}, f32[32,720]{1,0:T(8,128)S(1)}) fusion(bf16[32,2048]{1,0:T(8,128)(2,1)S(1)} %all_gather.3, bf16[720,2048]{1,0:T(8,128)(2,1)S(1)} %copy-done, bf16[32,720]{1,0:T(8,128)(2,1)} %param.21), kind=kOutput, calls=%fused_computation.48 | convolution fusion | flops 94510048 | bytes 3218560 | tf_op jit(solution)/shard_map/dot_general | solution.py:96
  25.6 7.5 %psum.7 = f32[32]{0:T(128)S(1)} all-reduce(f32[32]{0:T(128)S(1)} %get-tuple-element.11), channel_id=1, replica_groups=mesh['dp'=8,'expert'=4] {'expert'}, use_global_device_ids=true, to_apply=%region_5.6 | all-reduce | flops 32 | bytes 256 | tf_op jit(solution)/shard_map/psum | solution.py:109
  33.1 0.8 dynamic_slice.27
  33.9 0.4 convolution_convert_fusion
  34.3 16.2 %all_to_all.10 = bf16[8,32,720]{2,1,0:T(8,128)(2,1)S(1)} all-to-all(bf16[8,32,720]{2,1,0:T(8,128)(2,1)S(1)} %convolution_convert_fusion), channel_id=1, replica_groups=mesh['dp'=8,'expert'=4] {'dp'}, dimensions={0} | all-to-all | bytes 737280 | tf_op jit(solution)/shard_map/all_to_all | solution.py:120
  50.5 0.9 copy.35
  51.4 0.0 collective-permute-start.1
  51.4 1.7 %collective-permute-start = (bf16[256,720]{0,1:T(8,128)(2,1)}, bf16[256,720]{0,1:T(8,128)(2,1)S(1)}, u32[]{:S(2)}, u32[]{:S(2)}) collective-permute-start(bf16[256,720]{0,1:T(8,128)(2,1)} %copy.35), channel_id=1, source_target_pairs={{0,3},{1,0},{2,1},{3,2},{4,7},{5,4},{6,5},{7,6},{8,11},{9,8},{10,9... | collective-permute-start | bytes 1105928 | tf_op jit(solution)/shard_map/ppermute | solution.py:140
  53.2 2.7 %fusion.14 = f32[256,2,720]{0,2,1:T(8,128)S(1)} fusion(bf16[256,720,1]{1,0,2:T(8,128)(2,1)S(1)} %bitcast.66, bf16[1,2,720,2880]{3,2,1,0:T(8,128)(2,1)} %param.26, s32[]{:T(128)S(6)} %select_n.49), kind=kOutput, calls=%fused_computation.10 | convolution fusion | flops 530841600 | bytes 4055044 | tf_op jit(solution)/shard_map/rc,hfc->rhf/dot_general | solution.py:150
  55.9 4.9 %collective-permute-done.1 = bf16[256,720]{0,1:T(8,128)(2,1)} collective-permute-done((bf16[256,720]{0,1:T(8,128)(2,1)}, bf16[256,720]{0,1:T(8,128)(2,1)}, u32[]{:S(2)}, u32[]{:S(2)}) %collective-permute-start.1) | collective-permute-done | bytes 368672 | tf_op jit(solution)/shard_map/ppermute | solution.py:138
  60.8 0.3 collective-permute-start.2
  61.1 2.9 %fusion.10 = f32[256,2,720]{0,2,1:T(8,128)S(1)} fusion(bf16[1,2,720,2880]{3,2,1,0:T(8,128)(2,1)} %param.26, s32[]{:T(128)S(6)} %select_n.53, bf16[256,720]{0,1:T(8,128)(2,1)} %collective-permute-done.1), kind=kOutput, calls=%fused_computation.6 | convolution fusion | flops 530841600 | bytes 4055044 | tf_op jit(solution)/shard_map/rc,hfc->rhf/dot_general | solution.py:150
  64.0 0.0 collective-permute-done
  64.0 0.0 slice-start
  64.0 2.9 %fusion.12 = f32[256,2,720]{0,2,1:T(8,128)S(1)} fusion(bf16[1,2,720,2880]{3,2,1,0:T(8,128)(2,1)} %param.26, s32[]{:T(128)S(6)} %select_n.51, bf16[256,720]{0,1:T(8,128)(2,1)S(1)} %collective-permute-done), kind=kOutput, calls=%fused_computation.8 | convolution fusion | flops 530841600 | bytes 4055044 | tf_op jit(solution)/shard_map/rc,hfc->rhf/dot_general | solution.py:150
  66.9 0.0 slice-start.1
  66.9 1.0 collective-permute-done.2
  67.9 2.8 %add_add_fusion = f32[256,2,720]{0,2,1:T(8,128)S(1)} fusion(f32[256,2,720]{0,2,1:T(8,128)S(1)} %fusion.10, f32[256,2,720]{0,2,1:T(8,128)S(1)} %fusion.14, f32[256,2,720]{0,2,1:T(8,128)S(1)} %fusion.12, bf16[1,2,720,2880]{3,2,1,0:T(8,128)(2,1)} %param.26, s32[]{:T(128)S(6)} %select_n.55, bf16[256,720]{0,1:T(8,128)(2,1)S(1)} %collective-permute-done.2), kind=kOutput, calls=%fused_computation.16 | convolution fusion | flops 531947520 | bytes 8478724 | tf_op jit(solution)/shard_map/rc,hfc->rhf/dot_general | solution.py:150
  70.8 0.0 copy-start.3
  70.8 3.2 %fusion.5 = bf16[2880,256]{1,0:T(8,128)(2,1)} fusion(bf16[1,720,2880]{2,1,0:T(8,128)(2,1)S(1)} %bitcast.73, f32[256,2,720]{0,2,1:T(8,128)S(1)} %add_add_fusion), kind=kOutput, calls=%fused_computation.3 | convolution fusion | flops 1063895040 | bytes 7096320 | tf_op jit(solution)/shard_map/dot_general | solution.py:161
  74.0 0.0 reduce-scatter.2.cloned.1.call-update
  74.0 0.1 broadcast_in_dim.55
  74.1 0.1 and.38
  74.2 0.2 reduce_window_sum.18
  74.4 0.1 select_reduce_fusion
  74.5 0.1 mul.106
  74.6 26.7 %reduce-scatter.2.cloned.1.call-done = bf16[720,256]{1,0:T(8,128)(2,1)} async-done(((bf16[2880,256]{1,0:T(8,128)(2,1)}), bf16[720,256]{1,0:T(8,128)(2,1)}) %reduce-scatter.2.cloned.1.call-update) | async-done | bytes 368656 | tf_op jit(solution)/shard_map/reduce_scatter | solution.py:160
  101.3 1.8 %fusion.31 = bf16[256,720]{0,1:T(8,128)(2,1)} fusion(bf16[720,256]{1,0:T(8,128)(2,1)} %reduce-scatter.2.cloned.1.call-done, f32[256]{0:T(256)S(1)} %mul.106), kind=kLoop, calls=%fused_computation.33 | loop fusion | flops 552960 | bytes 738304 | tf_op jit(solution)/shard_map/transpose | solution.py:169
  103.1 1.2 copy.37
  104.3 17.3 %all_to_all.11 = bf16[8,32,720]{2,1,0:T(8,128)(2,1)S(1)} all-to-all(bf16[8,32,720]{2,1,0:T(8,128)(2,1)S(1)} %bitcast.68), channel_id=1, replica_groups=mesh['dp'=8,'expert'=4] {'dp'}, dimensions={0} | all-to-all | bytes 737280 | tf_op jit(solution)/shard_map/all_to_all | solution.py:170
  121.5 1.0 fusion.27
  (22 shorter events, 0.1 us)
Async XLA Ops:
  6.5 17.3 %copy-start = (bf16[720,2048]{1,0:T(8,128)(2,1)S(1)}, bf16[720,2048]{1,0:T(8,128)(2,1)}, u32[]{:S(2)}) copy-start(bf16[720,2048]{1,0:T(8,128)(2,1)} %param.22) | copy-start | bytes 8847364
  6.5 6.5 %copy-start.2 = (bf16[8,256]{1,0:T(8,128)(2,1)S(1)}, bf16[8,256]{1,0:T(8,128)(2,1)}, u32[]{:S(2)}) copy-start(bf16[8,256]{1,0:T(8,128)(2,1)} %param.15) | copy-start | bytes 12292
  6.5 7.2 %copy-start.4 = (f32[32]{0:T(128)S(1)}, f32[32]{0:T(128)}, u32[]{:S(2)}) copy-start(f32[32]{0:T(128)} %param.20) | copy-start | bytes 388
  6.5 94.8 %reduce-scatter.2.cloned.1.call-start = ((), (), s32[]{:S(2)}) async-start(), calls=%async_computation.3 | async-start | bytes 1843200 | tf_op jit(solution)/shard_map/reduce_scatter | solution.py:160
  8.7 14.8 %copy-start.1 = (s32[256,4]{0,1:T(4,128)S(1)}, s32[256,4]{0,1:T(4,128)}, u32[]{:S(2)}) copy-start(s32[256,4]{0,1:T(4,128)} %param.24) | copy-start | bytes 12292
  51.4 9.3 %collective-permute-start.1 = (bf16[256,720]{0,1:T(8,128)(2,1)}, bf16[256,720]{0,1:T(8,128)(2,1)}, u32[]{:S(2)}, u32[]{:S(2)}) collective-permute-start(bf16[256,720]{0,1:T(8,128)(2,1)} %copy.35), channel_id=1, source_target_pairs={{0,1},{1,2},{2,3},{3,0},{4,5},{5,6},{6,7},{7,4},{8,9},{9,10},{10,1... | collective-permute-start | bytes 1105928 | tf_op jit(solution)/shard_map/ppermute | solution.py:138
  51.4 12.5 %collective-permute-start = (bf16[256,720]{0,1:T(8,128)(2,1)}, bf16[256,720]{0,1:T(8,128)(2,1)S(1)}, u32[]{:S(2)}, u32[]{:S(2)}) collective-permute-start(bf16[256,720]{0,1:T(8,128)(2,1)} %copy.35), channel_id=1, source_target_pairs={{0,3},{1,0},{2,1},{3,2},{4,7},{5,4},{6,5},{7,6},{8,11},{9,8},{10,9... | collective-permute-start | bytes 1105928 | tf_op jit(solution)/shard_map/ppermute | solution.py:140
  60.8 7.1 %collective-permute-start.2 = (bf16[256,720]{0,1:T(8,128)(2,1)}, bf16[256,720]{0,1:T(8,128)(2,1)S(1)}, u32[]{:S(2)}, u32[]{:S(2)}) collective-permute-start(bf16[256,720]{0,1:T(8,128)(2,1)} %collective-permute-done.1), channel_id=1, source_target_pairs={{0,1},{1,2},{2,3},{3,0},{4,5},{5,6},{6,7},{7,4},{8,9},{9,10},{10,1... | collective-permute-start | bytes 1105928 | tf_op jit(solution)/shard_map/ppermute | solution.py:138
  64.0 6.8 %slice-start = ((s8[4239360]{0:T(1024)(128)(4,1)}), s8[4194304]{0:T(1024)(128)(4,1)S(1)}, s32[]{:S(2)}) async-start(s8[4239360]{0:T(1024)(128)(4,1)} %bitcast.72), calls=%async_computation.4 | async-start | bytes 8388608
  66.9 3.9 %slice-start.1 = ((s8[4239360]{0:T(1024)(128)(4,1)}), s8[45056]{0:T(1024)(128)(4,1)S(1)}, s32[]{:S(2)}) async-start(s8[4239360]{0:T(1024)(128)(4,1)} %bitcast.72), calls=%async_computation.5 | async-start | bytes 90112
  70.8 3.2 %copy-start.3 = (f32[256,4]{0,1:T(4,128)S(1)}, f32[256,4]{0,1:T(4,128)}, u32[]{:S(2)}) copy-start(f32[256,4]{0,1:T(4,128)} %param.25) | copy-start | bytes 12292
Sparse Core Ops, SparseCore 0:
  74.1 27.1 reduce-scatter.1
